TPU v7x, 32 devices: a whole 2x2x4 slice. The times are simulated.
32 devices in a mesh: row: 2 (over y), col: 4 (over x, core), rep: 4 (over z).
Axes of the slice: x: 2, y: 2, z: 4, core: 2. Of those that a mesh axis runs over, the one named last changes fastest.
Arguments:
- hidden: bfloat16 [512, 7168], P('rep'), may hold values from -6 to 6
- train_weight: bfloat16 [7168, 16384], P(('rep', 'row'), 'col'), may hold values from -0.0625 to 0.0625
- shard_order: int32 [4, 4, 2], replicated, may hold values from 0 to 1, each once within a row
Outputs:
- served_weight: bfloat16 [7168, 16384], P(None, ('col', 'row'))
- projected: float32 [512, 16384], P('rep', ('col', 'row'))
Inputs may be any that keep to these rules, and one draw needn't show every extreme that they name: Each shard_order[c, k] is a permutation of 0 to 1.
All inputs are finite; a program needn't handle non-finite values.
Results may differ from a plain program's by a relative error of at most 0.001.
Values may be sent and summed in bfloat16 or wider, within the bound.
A program may use at most 128 MiB of HBM per device.

v0:
```python
import jax
import jax.numpy as jnp
from jax import lax
from jax.sharding import PartitionSpec as P


def shards(hidden, train_weight, shard_order):
    row_count = lax.axis_size("row")
    rows_tile = train_weight.shape[0]
    cols_tile = train_weight.shape[1]
    piece_cols = cols_tile // row_count
    sub_count = shard_order.shape[1]
    sub_cols = piece_cols // sub_count
    my_order = lax.dynamic_index_in_dim(shard_order, lax.axis_index("col"), 0, keepdims=False)
    source_ids = lax.broadcasted_iota(jnp.int32, (sub_count, row_count, row_count), 2)
    selector = (my_order[:, :, None] == source_ids).astype(jnp.bfloat16)
    tiled = train_weight.reshape(rows_tile, row_count, sub_count, sub_cols)
    picked = jnp.einsum("ksj,rjkc->rskc", selector, tiled, preferred_element_type=jnp.float32)
    ordered = picked.astype(jnp.bfloat16).reshape(rows_tile, cols_tile)
    column = lax.all_to_all(ordered, "row", split_axis=1, concat_axis=0, tiled=True)
    served = lax.all_gather(column, "rep", axis=0, tiled=True)
    projected = jnp.dot(hidden, served, preferred_element_type=jnp.float32)
    return (served, projected)


def solution(mesh):
    placed = (P("rep", None), P(("rep", "row"), "col"), P())
    return jax.shard_map(
        shards,
        mesh=mesh,
        in_specs=placed,
        out_specs=(P(None, ("col", "row")), P("rep", ("col", "row"))),
        check_vma=False,
    )
```

profile of v0, /device:TPU:0, one launch (start us, length us, event | category | flops | bytes accessed | tf_op | source)
XLA Modules:
  0.0 697.5 jit_solution(17215963833131791758)
XLA Ops:
  7.2 0.0 copy-start
  7.2 0.0 all-gather.2.cloned.1.call-start
  7.2 0.8 dynamic-slice_bitcast_fusion
  8.0 0.1 copy.12
  8.1 12.8 %reshape.14 = bf16[896,2,4,512]{3,2,1,0:T(4,128)(2,1)} reshape(bf16[896,4096]{1,0:T(8,128)(2,1)} %param.4) | data formatting | bytes 14680064 | tf_op jit(solution)/shard_map/reshape | solution.py:17
  21.0 18.4 %fusion = bf16[896,2,4,512]{3,1,0,2:T(2,128)(2,1)} fusion(bf16[896,2,4,512]{3,2,1,0:T(4,128)(2,1)} %reshape.14, s32[4,2]{1,0:T(4,128)S(1)} %copy.12), kind=kOutput, calls=%fused_computation.1 | convolution fusion | flops 18350096 | bytes 14680096 | tf_op jit(solution)/shard_map/ksj,rjkc->rskc/dot_general | solution.py:18
  39.3 18.6 %copy.14 = bf16[896,2,4,512]{0,3,2,1:T(8,128)(2,1)} copy(bf16[896,2,4,512]{3,1,0,2:T(2,128)(2,1)} %fusion) | data formatting | bytes 14680064 | tf_op jit(solution)/shard_map/convert_element_type | solution.py:19
  57.9 92.8 %all_to_all.19 = bf16[896,2,2048]{0,2,1:T(8,128)(2,1)} all-to-all(bf16[896,2,2048]{0,2,1:T(8,128)(2,1)} %bitcast.17), channel_id=1, replica_groups=mesh['row'=2,'col'=4,'rep'=4] {'row'}, dimensions={1} | all-to-all | bytes 14680064 | tf_op jit(solution)/shard_map/all_to_all | solution.py:20
  150.8 11.3 %copy.15 = bf16[2,896,2048]{2,1,0:T(8,128)(2,1)} copy(bf16[2,896,2048]{1,2,0:T(8,128)(2,1)} %bitcast.18) | data formatting | bytes 14680064 | tf_op jit(solution)/shard_map/all_to_all | solution.py:20
  162.0 0.0 all-gather.2.cloned.1.call-update
  162.1 493.7 %all-gather.2.cloned.1.call-done = bf16[7168,2048]{1,0:T(8,128)(2,1)} async-done(((bf16[1792,2048]{1,0:T(8,128)(2,1)}), bf16[7168,2048]{1,0:T(8,128)(2,1)}) %all-gather.2.cloned.1.call-update) | async-done | bytes 29360144 | tf_op jit(solution)/shard_map/all_gather | solution.py:21
  655.8 0.0 copy-done
  655.8 13.3 %convolution_bitcast_fusion = f32[128,2048]{0,1:T(8,128)S(1)} fusion(bf16[7168,2048]{1,0:T(8,128)(2,1)} %all-gather.2.cloned.1.call-done, bf16[128,7168]{1,0:T(8,128)(2,1)S(1)} %copy-done), kind=kOutput, calls=%fused_computation.3 | convolution fusion | flops 3758096384 | bytes 32243712 | tf_op jit(solution)/shard_map/dot_general | solution.py:22
  669.1 1.3 copy.16
  670.4 0.0 copy-start.1
  670.4 20.2 %copy.21 = bf16[7168,2048]{1,0:T(8,128)(2,1)} copy(bf16[7168,2048]{1,0:T(8,128)(2,1)} %all-gather.2.cloned.1.call-done) | data formatting | bytes 58720256
  690.6 0.0 copy-done.1
Async XLA Ops:
  7.2 648.6 %copy-start = (bf16[128,7168]{1,0:T(8,128)(2,1)S(1)}, bf16[128,7168]{1,0:T(8,128)(2,1)}, u32[]{:S(2)}) copy-start(bf16[128,7168]{1,0:T(8,128)(2,1)} %param.3) | copy-start | bytes 5505028
  7.2 648.6 %all-gather.2.cloned.1.call-start = ((), (), s32[]{:S(2)}) async-start(), calls=%async_computation.1 | async-start | bytes 36700160 | tf_op jit(solution)/shard_map/all_gather | solution.py:21
  670.4 20.2 %copy-start.1 = (bf16[128,7168]{1,0:T(8,128)(2,1)S(1)}, bf16[128,7168]{1,0:T(8,128)(2,1)}, u32[]{:S(2)}) copy-start(bf16[128,7168]{1,0:T(8,128)(2,1)} %param.3) | copy-start | bytes 5505028
Sparse Core Ops, SparseCore 0:
  162.2 493.5 all-gather.1
where the time goes:
time: 699 us; the launch traced here: 697 us
  waiting for transfers between devices  494 us (71%)
  blocking collectives  92.8 us (13%)
  local copies, waits for them, and re-layouts  65.1 us (9%)
  matrix products  31.7 us (5%)
  between operations  14.1 us (2%)
    all_gather x1, waiting for transfers between devices, shards(): served = lax.all_gather(column, 'rep', axis=0, tiled=True)  494 us
    all_to_all x1, blocking collectives, shards(): lax.all_to_all(ordered, 'row', split_axis=1, concat_axis=0, tiled=True)  92.8 us
    unnamed x6, local copies, waits for them, and re-layouts  21.5 us
    convert_element_type x1, local copies, waits for them, and re-layouts, shards(): ordered = picked.astype(jnp.bfloat16).reshape(rows_tile, cols_tile)  18.6 us
    dot_general x1, matrix products, shards(): jnp.einsum('ksj,rjkc->rskc', selector, tiled, preferred_element_type=jnp....  18.4 us
  transfers between devices with their start and end apart: 1, of which 1 were waited for; matrix products, arithmetic and copies ran while one was open for 0% of the time, Pallas kernels for 0%

commit v1 on v0

--- a/solution.py
+++ b/solution.py
@@ -17,7 +17,10 @@
     tiled = train_weight.reshape(rows_tile, row_count, sub_count, sub_cols)
     picked = jnp.einsum("ksj,rjkc->rskc", selector, tiled, preferred_element_type=jnp.float32)
     ordered = picked.astype(jnp.bfloat16).reshape(rows_tile, cols_tile)
-    column = lax.all_to_all(ordered, "row", split_axis=1, concat_axis=0, tiled=True)
+    column = jnp.concatenate(
+        lax.all_to_all(jnp.stack(jnp.split(ordered, lax.axis_size("row"), axis=1)), "row", 0, 0),
+        axis=0,
+    )
     served = lax.all_gather(column, "rep", axis=0, tiled=True)
     projected = jnp.dot(hidden, served, preferred_element_type=jnp.float32)
     return (served, projected)

time: 699 us -> 701 us (level)
  no operation moved by 1% of the time
where the time goes in v1:
time: 701 us; the launch traced here: 700 us
  waiting for transfers between devices  494 us (70%)
  blocking collectives  86.8 us (12%)
  local copies, waits for them, and re-layouts  70.7 us (10%)
  matrix products  31.7 us (5%)
  between operations  14.1 us (2%)
    all_gather x1, waiting for transfers between devices, shards(): served = lax.all_gather(column, 'rep', axis=0, tiled=True)  494 us
    all_to_all x1, blocking collectives, shards(): lax.all_to_all(jnp.stack(jnp.split(ordered, lax.axis_size('row'), axis=1)...  86.8 us
    unnamed x6, local copies, waits for them, and re-layouts  21.5 us
    convert_element_type x1, local copies, waits for them, and re-layouts, shards(): ordered = picked.astype(jnp.bfloat16).reshape(rows_tile, cols_tile)  18.6 us
    dot_general x1, matrix products, shards(): jnp.einsum('ksj,rjkc->rskc', selector, tiled, preferred_element_type=jnp....  18.4 us
  transfers between devices with their start and end apart: 1, of which 1 were waited for; matrix products, arithmetic and copies ran while one was open for 0% of the time, Pallas kernels for 0%

profile of v1, /device:TPU:0, one launch (start us, length us, event | category | flops | bytes accessed | tf_op | source)
XLA Modules:
  0.0 699.8 jit_solution(5270363923930004330)
XLA Ops:
  7.2 0.0 copy-start
  7.2 0.0 all-gather.2.cloned.1.call-start
  7.2 0.8 dynamic-slice_bitcast_fusion
  8.0 0.1 copy.12
  8.1 12.8 %reshape.15 = bf16[896,2,4,512]{3,2,1,0:T(4,128)(2,1)} reshape(bf16[896,4096]{1,0:T(8,128)(2,1)} %param.4) | data formatting | bytes 14680064 | tf_op jit(solution)/shard_map/reshape | solution.py:17
  21.0 18.4 %fusion = bf16[896,2,4,512]{3,1,0,2:T(2,128)(2,1)} fusion(bf16[896,2,4,512]{3,2,1,0:T(4,128)(2,1)} %reshape.15, s32[4,2]{1,0:T(4,128)S(1)} %copy.12), kind=kOutput, calls=%fused_computation.1 | convolution fusion | flops 18350096 | bytes 14680096 | tf_op jit(solution)/shard_map/ksj,rjkc->rskc/dot_general | solution.py:18
  39.3 18.6 %copy.14 = bf16[896,2,4,512]{0,3,2,1:T(8,128)(2,1)} copy(bf16[896,2,4,512]{3,1,0,2:T(2,128)(2,1)} %fusion) | data formatting | bytes 14680064 | tf_op jit(solution)/shard_map/convert_element_type | solution.py:19
  57.9 5.5 slice_bitcast_fusion.1
  63.5 2.8 pad_maximum_fusion
  66.2 86.8 %all_to_all.5 = bf16[2,896,2048]{1,2,0:T(8,128)(2,1)} all-to-all(bf16[2,896,2048]{1,2,0:T(8,128)(2,1)S(1)} %pad_maximum_fusion), channel_id=1, replica_groups=mesh['row'=2,'col'=4,'rep'=4] {'row'}, dimensions={0} | all-to-all | bytes 14680064 | tf_op jit(solution)/shard_map/all_to_all | solution.py:21
  153.1 11.3 %copy.15 = bf16[2,896,2048]{2,1,0:T(8,128)(2,1)} copy(bf16[2,896,2048]{1,2,0:T(8,128)(2,1)} %all_to_all.5) | data formatting | bytes 14680064 | tf_op jit(solution)/shard_map/all_to_all | solution.py:21
  164.3 0.0 all-gather.2.cloned.1.call-update
  164.3 493.7 %all-gather.2.cloned.1.call-done = bf16[7168,2048]{1,0:T(8,128)(2,1)} async-done(((bf16[1792,2048]{1,0:T(8,128)(2,1)}), bf16[7168,2048]{1,0:T(8,128)(2,1)}) %all-gather.2.cloned.1.call-update) | async-done | bytes 29360144 | tf_op jit(solution)/shard_map/all_gather | solution.py:24
  658.1 0.0 copy-done
  658.1 13.3 %convolution_bitcast_fusion = f32[128,2048]{0,1:T(8,128)S(1)} fusion(bf16[7168,2048]{1,0:T(8,128)(2,1)} %all-gather.2.cloned.1.call-done, bf16[128,7168]{1,0:T(8,128)(2,1)S(1)} %copy-done), kind=kOutput, calls=%fused_computation.6 | convolution fusion | flops 3758096384 | bytes 32243712 | tf_op jit(solution)/shard_map/dot_general | solution.py:25
  671.4 1.3 copy.16
  672.7 0.0 copy-start.1
  672.7 20.2 %copy.21 = bf16[7168,2048]{1,0:T(8,128)(2,1)} copy(bf16[7168,2048]{1,0:T(8,128)(2,1)} %all-gather.2.cloned.1.call-done) | data formatting | bytes 58720256
  692.9 0.0 copy-done.1
Async XLA Ops:
  7.2 650.9 %copy-start = (bf16[128,7168]{1,0:T(8,128)(2,1)S(1)}, bf16[128,7168]{1,0:T(8,128)(2,1)}, u32[]{:S(2)}) copy-start(bf16[128,7168]{1,0:T(8,128)(2,1)} %param.3) | copy-start | bytes 5505028
  7.2 650.9 %all-gather.2.cloned.1.call-start = ((), (), s32[]{:S(2)}) async-start(), calls=%async_computation.1 | async-start | bytes 36700160 | tf_op jit(solution)/shard_map/all_gather | solution.py:24
  672.7 20.2 %copy-start.1 = (bf16[128,7168]{1,0:T(8,128)(2,1)S(1)}, bf16[128,7168]{1,0:T(8,128)(2,1)}, u32[]{:S(2)}) copy-start(bf16[128,7168]{1,0:T(8,128)(2,1)} %param.3) | copy-start | bytes 5505028
Sparse Core Ops, SparseCore 0:
  164.5 493.5 all-gather.1

commit v2 on v0

--- a/solution.py
+++ b/solution.py
@@ -18,7 +18,12 @@
     picked = jnp.einsum("ksj,rjkc->rskc", selector, tiled, preferred_element_type=jnp.float32)
     ordered = picked.astype(jnp.bfloat16).reshape(rows_tile, cols_tile)
     column = lax.all_to_all(ordered, "row", split_axis=1, concat_axis=0, tiled=True)
-    served = lax.all_gather(column, "rep", axis=0, tiled=True)
+    ring = [column]
+    for hop in range(3):
+        ring.append(lax.ppermute(ring[-1], "rep", [(dev, (dev + 1) % 4) for dev in range(4)]))
+    served = jnp.roll(
+        jnp.concatenate(ring[::-1], axis=0), (lax.axis_index("rep") + 1) * ring[0].shape[0], axis=0
+    )
     projected = jnp.dot(hidden, served, preferred_element_type=jnp.float32)
     return (served, projected)
 

time: 699 us -> 729 us (1.043)
  local copies, waits for them, and re-layouts: 65.1 us -> 122 us
  waiting for transfers between devices: 494 us -> 479 us
  between operations: 14.1 us -> 0.67 us
    all_gather x1 -> x0, waiting for transfers between devices: 494 us -> none  [shards(): served = lax.all_gather(column, 'rep', axis=0, tiled=True)]
    ppermute x0 -> x3, waiting for transfers between devices: none -> 479 us  [shards(): lax.ppermute(ring[-1], 'rep', [(dev, (dev + 1) % 4) for dev in range(4)])]
    unnamed x6 -> x16, local copies, waits for them, and re-layouts: 21.5 us -> 53.5 us
    dynamic_slice x0 -> x1, local copies, waits for them, and re-layouts: none -> 20.2 us  [shards(): jnp.roll(jnp.concatenate(ring[::-1], axis=0), (lax.axis_index('rep') + 1)...]
  transfers between devices with their start and end apart: 1 -> 3, of which waited for: 1 -> 3; matrix products, arithmetic and copies ran while one was open for 0% -> 0% of each run, Pallas kernels for 0% -> 0%
where the time goes in v2:
time: 729 us; the launch traced here: 728 us
  waiting for transfers between devices  479 us (66%)
  local copies, waits for them, and re-layouts  122 us (17%)
  blocking collectives  92.8 us (13%)
  matrix products  31.7 us (4%)
    ppermute x3, waiting for transfers between devices, shards(): lax.ppermute(ring[-1], 'rep', [(dev, (dev + 1) % 4) for dev in range(4)])  479 us
    all_to_all x1, blocking collectives, shards(): lax.all_to_all(ordered, 'row', split_axis=1, concat_axis=0, tiled=True)  92.8 us
    unnamed x16, local copies, waits for them, and re-layouts  53.5 us
    dynamic_slice x1, local copies, waits for them, and re-layouts, shards(): jnp.roll(jnp.concatenate(ring[::-1], axis=0), (lax.axis_index('rep') + 1)...  20.2 us
    convert_element_type x1, local copies, waits for them, and re-layouts, shards(): ordered = picked.astype(jnp.bfloat16).reshape(rows_tile, cols_tile)  18.6 us
    dot_general x1, matrix products, shards(): jnp.einsum('ksj,rjkc->rskc', selector, tiled, preferred_element_type=jnp....  18.3 us
  transfers between devices with their start and end apart: 3, of which 3 were waited for; matrix products, arithmetic and copies ran while one was open for 0% of the time, Pallas kernels for 0%

profile of v2, /device:TPU:0, one launch (start us, length us, event | category | flops | bytes accessed | tf_op | source)
XLA Modules:
  0.0 727.7 jit_solution(16830019995929481203)
XLA Ops:
  0.6 0.0 copy-start
  0.7 0.8 dynamic-slice_bitcast_fusion
  1.5 0.1 copy.12
  1.6 12.8 %reshape.14 = bf16[896,2,4,512]{3,2,1,0:T(4,128)(2,1)} reshape(bf16[896,4096]{1,0:T(8,128)(2,1)} %param.4) | data formatting | bytes 14680064 | tf_op jit(solution)/shard_map/reshape | solution.py:17
  14.4 18.3 %fusion = bf16[896,2,4,512]{3,1,0,2:T(2,128)(2,1)} fusion(bf16[896,2,4,512]{3,2,1,0:T(4,128)(2,1)} %reshape.14, s32[4,2]{1,0:T(4,128)S(1)} %copy.12), kind=kOutput, calls=%fused_computation.1 | convolution fusion | flops 18350096 | bytes 14680096 | tf_op jit(solution)/shard_map/ksj,rjkc->rskc/dot_general | solution.py:18
  32.7 18.6 %copy.14 = bf16[896,2,4,512]{0,3,2,1:T(8,128)(2,1)} copy(bf16[896,2,4,512]{3,1,0,2:T(2,128)(2,1)} %fusion) | data formatting | bytes 14680064 | tf_op jit(solution)/shard_map/convert_element_type | solution.py:19
  51.3 92.8 %all_to_all.19 = bf16[896,2,2048]{0,2,1:T(8,128)(2,1)} all-to-all(bf16[896,2,2048]{0,2,1:T(8,128)(2,1)} %bitcast.21), channel_id=1, replica_groups=mesh['row'=2,'col'=4,'rep'=4] {'row'}, dimensions={1} | all-to-all | bytes 14680064 | tf_op jit(solution)/shard_map/all_to_all | solution.py:20
  144.2 11.3 %copy.15 = bf16[2,896,2048]{2,1,0:T(8,128)(2,1)} copy(bf16[2,896,2048]{1,2,0:T(8,128)(2,1)} %bitcast.22) | data formatting | bytes 14680064 | tf_op jit(solution)/shard_map/all_to_all | solution.py:20
  155.4 1.7 collective-permute-start
  157.2 159.4 %collective-permute-done = bf16[1792,2048]{1,0:T(8,128)(2,1)S(1)} collective-permute-done((bf16[1792,2048]{1,0:T(8,128)(2,1)}, bf16[1792,2048]{1,0:T(8,128)(2,1)S(1)}, u32[]{:S(2)}, u32[]{:S(2)}) %collective-permute-start) | collective-permute-done | bytes 7340064 | tf_op jit(solution)/shard_map/ppermute | solution.py:23
  316.6 3.0 copy-done.1
  319.6 160.2 %collective-permute-done.1 = bf16[1792,2048]{1,0:T(8,128)(2,1)} collective-permute-done((bf16[1792,2048]{1,0:T(8,128)(2,1)S(1)}, bf16[1792,2048]{1,0:T(8,128)(2,1)}, u32[]{:S(2)}, u32[]{:S(2)}) %collective-permute-start.1) | collective-permute-done | bytes 7340064 | tf_op jit(solution)/shard_map/ppermute | solution.py:23
  479.8 159.5 %collective-permute-done.2 = bf16[1792,2048]{1,0:T(8,128)(2,1)} collective-permute-done((bf16[1792,2048]{1,0:T(8,128)(2,1)}, bf16[1792,2048]{1,0:T(8,128)(2,1)}, u32[]{:S(2)}, u32[]{:S(2)}) %collective-permute-start.2) | collective-permute-done | bytes 7340064 | tf_op jit(solution)/shard_map/ppermute | solution.py:23
  639.3 7.4 %constant_dynamic-update-slice_fusion.7 = bf16[14336,2048]{1,0:T(8,128)(2,1)} fusion(bf16[1792,2048]{1,0:T(8,128)(2,1)} %collective-permute-done.2), kind=kLoop, calls=%fused_computation.11 | loop fusion | bytes 14680064
  646.7 7.6 %constant_dynamic-update-slice_fusion.6 = bf16[14336,2048]{1,0:T(8,128)(2,1)} fusion(bf16[14336,2048]{1,0:T(8,128)(2,1)} %constant_dynamic-update-slice_fusion.7, bf16[1792,2048]{1,0:T(8,128)(2,1)} %collective-permute-done.1), kind=kLoop, calls=%fused_computation.10 | loop fusion | bytes 14680064
  654.4 7.4 %constant_dynamic-update-slice_fusion.5 = bf16[14336,2048]{1,0:T(8,128)(2,1)} fusion(bf16[14336,2048]{1,0:T(8,128)(2,1)} %constant_dynamic-update-slice_fusion.6, bf16[1792,2048]{1,0:T(8,128)(2,1)} %copy-done.1), kind=kLoop, calls=%fused_computation.9 | loop fusion | bytes 14680064
  661.8 4.3 constant_dynamic-update-slice_fusion.4
  666.1 7.5 %constant_dynamic-update-slice_fusion.3 = bf16[14336,2048]{1,0:T(8,128)(2,1)} fusion(bf16[14336,2048]{1,0:T(8,128)(2,1)} %constant_dynamic-update-slice_fusion.4, bf16[1792,2048]{1,0:T(8,128)(2,1)} %collective-permute-done.2), kind=kLoop, calls=%fused_computation.7 | loop fusion | bytes 14680064
  673.6 7.5 %constant_dynamic-update-slice_fusion.2 = bf16[14336,2048]{1,0:T(8,128)(2,1)} fusion(bf16[14336,2048]{1,0:T(8,128)(2,1)} %constant_dynamic-update-slice_fusion.3, bf16[1792,2048]{1,0:T(8,128)(2,1)} %collective-permute-done.1), kind=kLoop, calls=%fused_computation.6 | loop fusion | bytes 14680064
  681.1 7.4 %constant_dynamic-update-slice_fusion.1 = bf16[14336,2048]{1,0:T(8,128)(2,1)} fusion(bf16[14336,2048]{1,0:T(8,128)(2,1)} %constant_dynamic-update-slice_fusion.2, bf16[1792,2048]{1,0:T(8,128)(2,1)} %copy-done.1), kind=kLoop, calls=%fused_computation.5 | loop fusion | bytes 14680064
  688.5 4.3 constant_dynamic-update-slice_fusion
  692.8 20.2 %constant_dynamic-slice_fusion = bf16[7168,2048]{1,0:T(8,128)(2,1)} fusion(bf16[14336,2048]{1,0:T(8,128)(2,1)} %constant_dynamic-update-slice_fusion, s32[]{:T(128)S(6)} %select_n.19), kind=kLoop, calls=%fused_computation.16 | loop fusion | bytes 58720260 | tf_op jit(solution)/shard_map/jit(_roll_dynamic)/dynamic_slice | solution.py:24
  713.0 13.3 %convolution_bitcast_fusion = f32[128,2048]{0,1:T(8,128)S(1)} fusion(bf16[7168,2048]{1,0:T(8,128)(2,1)} %constant_dynamic-slice_fusion, bf16[128,7168]{1,0:T(8,128)(2,1)S(1)} %copy-done), kind=kOutput, calls=%fused_computation.3 | convolution fusion | flops 3758096384 | bytes 32243712 | tf_op jit(solution)/shard_map/dot_general | solution.py:27
  726.4 1.3 copy.16
  (9 shorter events, 0.0 us)
Async XLA Ops:
  0.6 712.4 %copy-start = (bf16[128,7168]{1,0:T(8,128)(2,1)S(1)}, bf16[128,7168]{1,0:T(8,128)(2,1)}, u32[]{:S(2)}) copy-start(bf16[128,7168]{1,0:T(8,128)(2,1)} %param.3) | copy-start | bytes 5505028
  155.4 161.2 %collective-permute-start = (bf16[1792,2048]{1,0:T(8,128)(2,1)}, bf16[1792,2048]{1,0:T(8,128)(2,1)S(1)}, u32[]{:S(2)}, u32[]{:S(2)}) collective-permute-start(bf16[1792,2048]{1,0:T(8,128)(2,1)} %bitcast.16), channel_id=1, source_target_pairs={{0,1},{1,2},{2,3},{3,0},{4,5},{5,6},{6,7},{7,4},{8,9},{9,10},{10,1... | collective-permute-start | bytes 22020104 | tf_op jit(solution)/shard_map/ppermute | solution.py:23
  316.6 3.0 copy-start.1
  319.6 160.2 %collective-permute-start.1 = (bf16[1792,2048]{1,0:T(8,128)(2,1)S(1)}, bf16[1792,2048]{1,0:T(8,128)(2,1)}, u32[]{:S(2)}, u32[]{:S(2)}) collective-permute-start(bf16[1792,2048]{1,0:T(8,128)(2,1)S(1)} %collective-permute-done), channel_id=1, source_target_pairs={{0,1},{1,2},{2,3},{3,0},{4,5},{5,6},{6,7},{7,4},{8,9},{9,10},{10,1... | collective-permute-start | bytes 22020104 | tf_op jit(solution)/shard_map/ppermute | solution.py:23
  479.8 159.6 %collective-permute-start.2 = (bf16[1792,2048]{1,0:T(8,128)(2,1)}, bf16[1792,2048]{1,0:T(8,128)(2,1)}, u32[]{:S(2)}, u32[]{:S(2)}) collective-permute-start(bf16[1792,2048]{1,0:T(8,128)(2,1)} %collective-permute-done.1), channel_id=1, source_target_pairs={{0,1},{1,2},{2,3},{3,0},{4,5},{5,6},{6,7},{7,4},{8,9},{9,10},{10,1... | collective-permute-start | bytes 22020104 | tf_op jit(solution)/shard_map/ppermute | solution.py:23
  479.8 182.0 %slice-start = ((s8[7340032]{0:T(1024)(128)(4,1)}), s8[4194304]{0:T(1024)(128)(4,1)S(1)}, s32[]{:S(2)}) async-start(s8[7340032]{0:T(1024)(128)(4,1)} %bitcast.17), calls=%async_computation.1 | async-start | bytes 8388608
  646.7 15.0 %slice-start.1 = ((s8[7340032]{0:T(1024)(128)(4,1)}), s8[3145728]{0:T(1024)(128)(4,1)S(1)}, s32[]{:S(2)}) async-start(s8[7340032]{0:T(1024)(128)(4,1)} %bitcast.17), calls=%async_computation.2 | async-start | bytes 6291456
